TPU v7x, 32 devices: a whole 2x2x4 slice. The times are simulated.
32 devices in a mesh: tok: 8 (over z, y), unit: 4 (over x, core).
Axes of the slice: x: 2, y: 2, z: 4, core: 2. Of those that a mesh axis runs over, the one named last changes fastest.
Arguments:
- act_a: bfloat16 [16384, 3072], P('tok', 'unit'), may hold values from -4000 to 4000
- act_b: bfloat16 [16384, 3072], P(('tok', 'unit')), may hold values from -4000 to 4000
Outputs:
- correlation: float32 [3072, 3072], P('tok', 'unit')
All inputs are finite; a program needn't handle non-finite values.
Results may differ from a plain program's by a relative error of at most 0.0003.
Values may be sent and summed in bfloat16 or wider, within the bound.
A program may use at most 128 MiB of HBM per device.

v0:
```python
import jax
import jax.numpy as jnp
from jax import lax
from jax.sharding import PartitionSpec as P


def contract_tokens(left, right):
    return lax.dot_general(
        left, right, (((0,), (0,)), ((), ())), preferred_element_type=jnp.float32
    )


def per_device(act_a, act_b):
    token_rows, own_units = act_a.shape
    units = act_b.shape[1]
    groups = lax.axis_size("tok")
    band = units // groups
    total_tokens = token_rows * groups
    wide_a = act_a.astype(jnp.float32)
    first_total = jnp.sum(wide_a, axis=0)
    first_square = jnp.sum(wide_a * wide_a, axis=0)
    piece = lax.all_gather(act_b, "unit", axis=0, tiled=True)
    product = contract_tokens(piece, act_a)
    wide_piece = piece.astype(jnp.float32)
    second_total = jnp.sum(wide_piece, axis=0)
    second_square = jnp.sum(wide_piece * wide_piece, axis=0)
    product, second_total, second_square = (product, second_total, second_square)
    shares = lax.psum_scatter(product, "tok", scatter_dimension=0, tiled=True)
    first_all, first_square_all, second_all, second_square_all = lax.psum(
        (first_total, first_square, second_total, second_square), "tok"
    )
    offset = lax.axis_index("tok") * band
    second_own = lax.dynamic_slice_in_dim(second_all, offset, band, 0)
    second_square_own = lax.dynamic_slice_in_dim(second_square_all, offset, band, 0)
    mean_a = first_all / total_tokens
    var_a = first_square_all / total_tokens - mean_a * mean_a
    mean_b = second_own / total_tokens
    var_b = second_square_own / total_tokens - mean_b * mean_b
    centered = shares / total_tokens - mean_b[:, None] * mean_a[None, :]
    return centered / (jnp.sqrt(var_b + 1e-05)[:, None] * jnp.sqrt(var_a + 1e-05)[None, :])


def solution(mesh):
    placed = (P("tok", "unit"), P(("tok", "unit"), None))
    return jax.shard_map(
        per_device, mesh=mesh, in_specs=placed, out_specs=P("tok", "unit"), check_vma=False
    )
```

profile of v0, /device:TPU:0, one launch (start us, length us, event | category | flops | bytes accessed | tf_op | source)
XLA Modules:
  0.0 281.4 jit_solution(8721838583599671117)
XLA Ops:
  6.5 0.0 copy-start
  6.5 0.0 all-gather.2.cloned.1.call-start
  6.5 0.7 all-gather.2.cloned.1.call-update
  7.3 0.0 reduce-scatter.2.cloned.1.call-start
  7.3 86.4 %all-gather.2.cloned.1.call-done = bf16[2048,3072]{1,0:T(8,128)(2,1)} async-done(((bf16[512,3072]{1,0:T(8,128)(2,1)}), bf16[2048,3072]{1,0:T(8,128)(2,1)}) %all-gather.2.cloned.1.call-update) | async-done | bytes 12582928 | tf_op jit(solution)/shard_map/all_gather | solution.py:22
  93.7 0.0 copy-done
  93.7 15.2 %fusion.2 = f32[3072,768]{1,0:T(8,128)} fusion(bf16[2048,3072]{1,0:T(8,128)(2,1)} %all-gather.2.cloned.1.call-done, bf16[2048,768]{1,0:T(8,128)(2,1)S(1)} %copy-done), kind=kOutput, calls=%fused_computation.11 | convolution fusion | flops 9663676416 | bytes 25165824 | tf_op jit(solution)/shard_map/dot_general | solution.py:8
  109.0 0.0 reduce-scatter.2.cloned.1.call-update
  109.0 0.9 convert_reduce_fusion.1
  109.9 8.0 %convert_reduce_fusion = (f32[3072]{0:T(1024)S(1)}, f32[3072]{0:T(1024)S(1)}) fusion(bf16[2048,3072]{1,0:T(8,128)(2,1)} %all-gather.2.cloned.1.call-done), kind=kLoop, calls=%fused_computation.1 | loop fusion | flops 25159680 | bytes 12607488 | tf_op jit(solution)/shard_map/reduce_sum | solution.py:25
  117.9 39.5 %all-reduce = (f32[768]{0:T(1024)S(1)}, f32[768]{0:T(1024)S(1)}, f32[3072]{0:T(1024)S(1)}, f32[3072]{0:T(1024)S(1)}) all-reduce(f32[768]{0:T(1024)S(1)} %get-tuple-element.8, f32[768]{0:T(1024)S(1)} %get-tuple-element.7, f32[3072]{0:T(1024)S(1)} %get-tuple-element.6, ...), channel_id=1, replica_groups=mesh['tok'=8,'unit'=4] {'tok'}, use_global_device_ids=true, to_apply=%region_8.0 | all-reduce | flops 7680 | bytes 61440 | tf_op jit(solution)/shard_map/psum | solution.py:29
  157.3 0.1 dynamic-slice_multiply_fusion
  157.4 114.6 %reduce-scatter.2.cloned.1.call-done = f32[384,768]{1,0:T(8,128)} async-done(((f32[3072,768]{1,0:T(8,128)}), f32[384,768]{1,0:T(8,128)}) %reduce-scatter.2.cloned.1.call-update) | async-done | bytes 1179664 | tf_op jit(solution)/shard_map/reduce_scatter | solution.py:28
  272.0 2.6 multiply_divide_fusion
  (1 shorter events, 0.0 us)
Async XLA Ops:
  6.5 87.2 %copy-start = (bf16[2048,768]{1,0:T(8,128)(2,1)S(1)}, bf16[2048,768]{1,0:T(8,128)(2,1)}, u32[]{:S(2)}) copy-start(bf16[2048,768]{1,0:T(8,128)(2,1)} %param.2) | copy-start | bytes 9437188
  6.5 87.2 %all-gather.2.cloned.1.call-start = ((), (), s32[]{:S(2)}) async-start(), calls=%async_computation.1 | async-start | bytes 15728640 | tf_op jit(solution)/shard_map/all_gather | solution.py:22
  7.3 264.7 %reduce-scatter.2.cloned.1.call-start = ((), (), s32[]{:S(2)}) async-start(), calls=%async_computation.2 | async-start | bytes 10616832 | tf_op jit(solution)/shard_map/reduce_scatter | solution.py:28
Sparse Core Ops, SparseCore 0:
  8.9 84.7 all-gather.1
  109.1 162.8 reduce-scatter.1
where the time goes:
time: 282 us; the launch traced here: 281 us
  waiting for transfers between devices  202 us (72%)
  blocking collectives  39.5 us (14%)
  matrix products  15.2 us (5%)
  between operations  13.4 us (5%)
  other arithmetic  11.5 us (4%)
    reduce_scatter x1, waiting for transfers between devices, per_device(): shares = lax.psum_scatter(product, 'tok', scatter_dimension=0, tiled=True)  115 us
    all_gather x1, waiting for transfers between devices, per_device(): piece = lax.all_gather(act_b, 'unit', axis=0, tiled=True)  86.4 us
    psum x1, blocking collectives, per_device(): lax.psum((first_total, first_square, second_total, second_square), 'tok')  39.5 us
    dot_general x1, matrix products, contract_tokens(): lax.dot_general(left, right, (((0,), (0,)), ((), ())), preferred_element_...  15.2 us
    reduce_sum x1, other arithmetic, per_device(): second_total = jnp.sum(wide_piece, axis=0)  8 us
  transfers between devices with their start and end apart: 2, of which 2 were waited for; matrix products, arithmetic and copies ran while one was open for 3% of the time, Pallas kernels for 0%

commit v1 on v0

--- a/solution.py
+++ b/solution.py
@@ -19,7 +19,9 @@
     wide_a = act_a.astype(jnp.float32)
     first_total = jnp.sum(wide_a, axis=0)
     first_square = jnp.sum(wide_a * wide_a, axis=0)
-    piece = lax.all_gather(act_b, "unit", axis=0, tiled=True)
+    piece = jnp.concatenate(
+        lax.all_to_all(jnp.stack([act_b] * lax.axis_size("unit")), "unit", 0, 0), axis=0
+    )
     product = contract_tokens(piece, act_a)
     wide_piece = piece.astype(jnp.float32)
     second_total = jnp.sum(wide_piece, axis=0)

time: 282 us -> 349 us (1.24)
  blocking collectives: 39.5 us -> 184 us
  waiting for transfers between devices: 202 us -> 115 us
  local copies, waits for them, and re-layouts: 0.01 us -> 12.6 us
    all_to_all x0 -> x1, blocking collectives: none -> 143 us  [per_device(): lax.all_to_all(jnp.stack([act_b] * lax.axis_size('unit')), 'unit', 0, 0)]
    all_gather x1 -> x0, waiting for transfers between devices: 86.4 us -> none  [per_device(): piece = lax.all_gather(act_b, 'unit', axis=0, tiled=True)]
    another operation x0 -> x1, local copies, waits for them, and re-layouts: none -> 8.06 us  [per_device(): jnp.stack([act_b] * lax.axis_size('unit'))]
    unnamed x2 -> x4, local copies, waits for them, and re-layouts: 0.01 us -> 4.57 us
  transfers between devices with their start and end apart: 2 -> 1, of which waited for: 2 -> 1; matrix products, arithmetic and copies ran while one was open for 3% -> 3% of each run, Pallas kernels for 0% -> 0%
where the time goes in v1:
time: 349 us
  blocking collectives  184 us (53%)
  waiting for transfers between devices  115 us (33%)
  between operations  13.4 us (4%)
  matrix products  12.9 us (4%)
  local copies, waits for them, and re-layouts  12.6 us (4%)
  other arithmetic  11.5 us (3%)
    all_to_all x1, blocking collectives, per_device(): lax.all_to_all(jnp.stack([act_b] * lax.axis_size('unit')), 'unit', 0, 0)  143 us
    reduce_scatter x1, waiting for transfers between devices, per_device(): shares = lax.psum_scatter(product, 'tok', scatter_dimension=0, tiled=True)  115 us
    psum x1, blocking collectives, per_device(): lax.psum((first_total, first_square, second_total, second_square), 'tok')  40.6 us
    dot_general x1, matrix products, contract_tokens(): lax.dot_general(left, right, (((0,), (0,)), ((), ())), preferred_element_...  12.9 us
    another operation x1, local copies, waits for them, and re-layouts, per_device(): jnp.stack([act_b] * lax.axis_size('unit'))  8.06 us
    reduce_sum x1, other arithmetic, per_device(): second_total = jnp.sum(wide_piece, axis=0)  8 us
  transfers between devices with their start and end apart: 1, of which 1 were waited for; matrix products, arithmetic and copies ran while one was open for 3% of the time, Pallas kernels for 0%

profile of v1, /device:TPU:0, one launch (start us, length us, event | category | flops | bytes accessed | tf_op | source)
XLA Modules:
  0.0 349.2 jit_solution(13224129377873912550)
XLA Ops:
  6.5 0.0 reduce-scatter.2.cloned.1.call-start
  6.5 8.1 %stack.2 = bf16[4,512,3072]{2,1,0:T(8,128)(2,1)} broadcast(bf16[512,3072]{1,0:T(8,128)(2,1)} %param.3), dimensions={1,2} | broadcast | bytes 15728640 | tf_op jit(solution)/shard_map/stack | solution.py:23
  14.6 0.0 copy-start.1
  14.6 143.4 %all_to_all.5 = bf16[4,512,3072]{2,1,0:T(8,128)(2,1)S(1)} all-to-all(bf16[4,512,3072]{2,1,0:T(8,128)(2,1)} %stack.2), channel_id=1, replica_groups=mesh['tok'=8,'unit'=4] {'unit'}, dimensions={0} | all-to-all | bytes 25165824 | tf_op jit(solution)/shard_map/all_to_all | solution.py:23
  158.0 0.0 copy-start
  158.0 4.6 %copy-done = bf16[4,512,3072]{2,1,0:T(8,128)(2,1)} copy-done((bf16[4,512,3072]{2,1,0:T(8,128)(2,1)}, bf16[4,512,3072]{2,1,0:T(8,128)(2,1)S(1)}, u32[]{:S(2)}) %copy-start) | copy-done | bytes 12582936
  162.6 0.0 copy-done.1
  162.6 12.9 %fusion.2 = f32[3072,768]{1,0:T(8,128)} fusion(bf16[2048,3072]{1,0:T(8,128)(2,1)S(1)} %bitcast.3, bf16[2048,768]{1,0:T(8,128)(2,1)S(1)} %copy-done.1), kind=kOutput, calls=%fused_computation.11 | convolution fusion | flops 9663676416 | bytes 25165824 | tf_op jit(solution)/shard_map/dot_general | solution.py:8
  175.5 0.0 reduce-scatter.2.cloned.1.call-update
  175.5 0.9 convert_reduce_fusion.1
  176.4 8.0 %convert_reduce_fusion = (f32[3072]{0:T(1024)S(1)}, f32[3072]{0:T(1024)S(1)}) fusion(bf16[4,512,3072]{2,1,0:T(8,128)(2,1)} %copy-done), kind=kLoop, calls=%fused_computation.1 | loop fusion | flops 25159680 | bytes 12607488 | tf_op jit(solution)/shard_map/reduce_sum | solution.py:27
  184.4 40.6 %all-reduce = (f32[768]{0:T(1024)S(1)}, f32[768]{0:T(1024)S(1)}, f32[3072]{0:T(1024)S(1)}, f32[3072]{0:T(1024)S(1)}) all-reduce(f32[768]{0:T(1024)S(1)} %get-tuple-element.8, f32[768]{0:T(1024)S(1)} %get-tuple-element.7, f32[3072]{0:T(1024)S(1)} %get-tuple-element.6, ...), channel_id=1, replica_groups=mesh['tok'=8,'unit'=4] {'tok'}, use_global_device_ids=true, to_apply=%region_8.0 | all-reduce | flops 7680 | bytes 61440 | tf_op jit(solution)/shard_map/psum | solution.py:31
  225.0 0.1 dynamic-slice_multiply_fusion
  225.1 114.7 %reduce-scatter.2.cloned.1.call-done = f32[384,768]{1,0:T(8,128)} async-done(((f32[3072,768]{1,0:T(8,128)}), f32[384,768]{1,0:T(8,128)}) %reduce-scatter.2.cloned.1.call-update) | async-done | bytes 1179664 | tf_op jit(solution)/shard_map/reduce_scatter | solution.py:30
  339.7 2.6 multiply_divide_fusion
  (1 shorter events, 0.0 us)
Async XLA Ops:
  6.5 333.2 %reduce-scatter.2.cloned.1.call-start = ((), (), s32[]{:S(2)}) async-start(), calls=%async_computation.2 | async-start | bytes 10616832 | tf_op jit(solution)/shard_map/reduce_scatter | solution.py:30
  14.6 148.0 %copy-start.1 = (bf16[2048,768]{1,0:T(8,128)(2,1)S(1)}, bf16[2048,768]{1,0:T(8,128)(2,1)}, u32[]{:S(2)}) copy-start(bf16[2048,768]{1,0:T(8,128)(2,1)} %param.2) | copy-start | bytes 9437188
  158.0 4.6 %copy-start = (bf16[4,512,3072]{2,1,0:T(8,128)(2,1)}, bf16[4,512,3072]{2,1,0:T(8,128)(2,1)S(1)}, u32[]{:S(2)}) copy-start(bf16[4,512,3072]{2,1,0:T(8,128)(2,1)S(1)} %all_to_all.5) | copy-start | bytes 37748740
Sparse Core Ops, SparseCore 0:
  175.6 164.0 reduce-scatter.1
